TPU v7x, 256 devices: a whole 4x4x8 slice. The times are simulated.
256 devices in a mesh: dp: 8 (over x, z_hi), ts: 32 (over z_lo, y, core).
Axes of the slice: x: 4, y: 4, z: 8 (z_hi: 2, z_lo: 4; z = z_hi * 4 + z_lo), core: 2. Of those that a mesh axis runs over, the one named last changes fastest.
Arguments:
- clip_video: bfloat16 [512, 4, 40, 128], P(('dp', 'ts')), may hold values from -6 to 6
- conv_weight: bfloat16 [3, 3, 3, 128, 128], replicated, may hold values from -0.109375 to 0.109375
- embed_weight: bfloat16 [128, 5120], replicated, may hold values from -0.5 to 0.5
- gain_spatial: float32 [5120], replicated, may hold values from 0.5 to 1.5
- gain_temporal: float32 [5120], replicated, may hold values from 0.5 to 1.5
- input_spatial: bfloat16 [5120, 384], P(('dp', 'ts')), may hold values from -0.078125 to 0.078125
- input_temporal: bfloat16 [5120, 384], P(('dp', 'ts')), may hold values from -0.078125 to 0.078125
- output_spatial: bfloat16 [128, 5120], replicated, may hold values from -2 to 2
- output_temporal: bfloat16 [128, 5120], replicated, may hold values from -2 to 2
- cotangent: bfloat16 [512, 4, 40, 5120], P(('dp', 'ts')), may hold values from -6 to 6
Outputs:
- layer_output: bfloat16 [512, 4, 40, 5120], P(('dp', 'ts'))
- grad_spatial: float32 [5120, 384], P(('dp', 'ts'))
All inputs are finite; a program needn't handle non-finite values.
Results may differ from a plain program's by a relative error of at most 0.015.
Values may be sent and summed in bfloat16 or wider, within the bound.
No kernel may reach another device: no remote copies, remote signals or barrier semaphores. Data moves between devices by JAX's collectives and lax.ppermute only.
A program may use at most 128 MiB of HBM per device.

v0:
```python
import jax
import jax.numpy as jnp
from jax import lax
from jax.sharding import PartitionSpec as P

FR = 16
epsilon = 1e-06
masked = -1e30


def passed_along(block, axis, distance):
    devices = range(lax.axis_size(axis))
    route = [(i - distance, i) for i in devices if i - distance in devices]
    return lax.ppermute(block, axis, route)


def side_by_side(arrays, axis, dim, along):
    widths = [a.shape[along] for a in arrays]
    both = jnp.concatenate(arrays, axis=along)
    whole = lax.all_gather(both, axis, axis=dim, tiled=True)
    return tuple(jnp.split(whole, [sum(widths[:k]) for k in range(1, len(widths))], axis=along))


def in_blocks(value, dim, size):
    dims = value.shape
    parts = value.reshape(*dims[:dim], size, dims[dim] // size, *dims[dim + 1 :])
    return jnp.moveaxis(parts, dim, 0)


def sum_at_owner(value, axis, dim):
    parts = in_blocks(value, dim, lax.axis_size(axis))
    arrived = lax.all_to_all(parts, axis, split_axis=0, concat_axis=0, tiled=True)
    return arrived.astype(jnp.float32).sum(axis=0)


def conv_local(volume, weight, count):
    frames, height, columns, channels = volume.shape
    out_channels = weight.shape[-1]
    padded = jnp.pad(volume, ((0, 0), (1, 1), (1, 1), (0, 0)))
    summed = jnp.zeros((count * height * columns, out_channels), jnp.float32)
    for time_tap in range(3):
        for row_tap in range(3):
            for col_tap in range(3):
                window = padded[
                    2 - time_tap : 2 - time_tap + count,
                    row_tap : row_tap + height,
                    col_tap : col_tap + columns,
                    :,
                ]
                summed = summed + jnp.dot(
                    window.reshape(-1, channels),
                    weight[time_tap, row_tap, col_tap],
                    preferred_element_type=jnp.float32,
                )
    return summed.reshape(count, height, columns, out_channels)


def rms_norm(hidden, norm_gain):
    widened = hidden.astype(jnp.float32)
    factor = lax.rsqrt(jnp.mean(widened * widened, axis=-1, keepdims=True) + epsilon)
    return ((widened * factor * norm_gain).astype(jnp.bfloat16), factor)


def rms_norm_grad(hidden, norm_gain, factor, upstream):
    widened = hidden.astype(jnp.float32)
    scaled = upstream * norm_gain
    inner_mean = jnp.mean(widened * scaled, axis=-1, keepdims=True)
    return factor * scaled - widened * factor**3 * inner_mean


def frame_forward(packed):
    frames, places, triple = packed.shape
    head_size = triple // 3
    queries = packed[..., :head_size]
    key_rows = packed[..., head_size : 2 * head_size]
    values = packed[..., 2 * head_size :]
    scores = jnp.einsum(
        "fqd,fkd->fqk", queries, key_rows, preferred_element_type=jnp.float32
    ) * head_size ** (-0.5)
    attend = jax.nn.softmax(scores, axis=-1)
    rounded = attend.astype(jnp.bfloat16)
    mixture = jnp.einsum("fqk,fkd->fqd", rounded, values, preferred_element_type=jnp.float32)
    return (mixture.astype(jnp.bfloat16), attend)


def frame_backward(packed, attend, upstream):
    frames, places, triple = packed.shape
    head_size = triple // 3
    scale_factor = head_size ** (-0.5)
    queries = packed[..., :head_size]
    key_rows = packed[..., head_size : 2 * head_size]
    values = packed[..., 2 * head_size :]
    rounded = attend.astype(jnp.bfloat16)
    grad_attend = jnp.einsum("fqd,fkd->fqk", upstream, values, preferred_element_type=jnp.float32)
    grad_values = jnp.einsum("fqk,fqd->fkd", rounded, upstream, preferred_element_type=jnp.float32)
    grad_scores = attend * (grad_attend - jnp.sum(grad_attend * attend, axis=-1, keepdims=True))
    grad_rounded = grad_scores.astype(jnp.bfloat16)
    grad_queries = (
        jnp.einsum("fqk,fkd->fqd", grad_rounded, key_rows, preferred_element_type=jnp.float32)
        * scale_factor
    )
    grad_keys = (
        jnp.einsum("fqk,fqd->fkd", grad_rounded, queries, preferred_element_type=jnp.float32)
        * scale_factor
    )
    joined = jnp.concatenate([grad_queries, grad_keys, grad_values], axis=-1)
    return joined.astype(jnp.bfloat16)


def clip_forward(packed):
    frames, places, triple = packed.shape
    head_size = triple // 3
    volume = packed.reshape(frames // FR, FR, places, triple)
    queries = volume[..., :head_size]
    key_rows = volume[..., head_size : 2 * head_size]
    values = volume[..., 2 * head_size :]
    scores = jnp.einsum(
        "cqpd,ckpd->cpqk", queries, key_rows, preferred_element_type=jnp.float32
    ) * head_size ** (-0.5)
    allowed = jnp.arange(FR)[:, None] >= jnp.arange(FR)[None, :]
    scores = jnp.where(allowed, scores, masked)
    attend = jax.nn.softmax(scores, axis=-1)
    rounded = attend.astype(jnp.bfloat16)
    mixture = jnp.einsum("cpqk,ckpd->cqpd", rounded, values, preferred_element_type=jnp.float32)
    return (mixture.astype(jnp.bfloat16).reshape(frames, places, head_size), attend)


def clip_backward(packed, attend, upstream):
    frames, places, triple = packed.shape
    head_size = triple // 3
    scale_factor = head_size ** (-0.5)
    volume = packed.reshape(frames // FR, FR, places, triple)
    queries = volume[..., :head_size]
    key_rows = volume[..., head_size : 2 * head_size]
    values = volume[..., 2 * head_size :]
    grad_out = upstream.reshape(frames // FR, FR, places, head_size)
    rounded = attend.astype(jnp.bfloat16)
    grad_attend = jnp.einsum(
        "cqpd,ckpd->cpqk", grad_out, values, preferred_element_type=jnp.float32
    )
    grad_values = jnp.einsum(
        "cpqk,cqpd->ckpd", rounded, grad_out, preferred_element_type=jnp.float32
    )
    grad_scores = attend * (grad_attend - jnp.sum(grad_attend * attend, axis=-1, keepdims=True))
    grad_rounded = grad_scores.astype(jnp.bfloat16)
    grad_queries = (
        jnp.einsum("cpqk,ckpd->cqpd", grad_rounded, key_rows, preferred_element_type=jnp.float32)
        * scale_factor
    )
    grad_keys = (
        jnp.einsum("cpqk,cqpd->ckpd", grad_rounded, queries, preferred_element_type=jnp.float32)
        * scale_factor
    )
    joined = jnp.concatenate([grad_queries, grad_keys, grad_values], axis=-1)
    return joined.astype(jnp.bfloat16).reshape(frames, places, triple)


def shards(
    clip_video,
    conv_weight,
    embed_weight,
    gain_spatial,
    gain_temporal,
    input_spatial,
    input_temporal,
    output_spatial,
    output_temporal,
    cotangent,
):
    frames_here = clip_video.shape[0]
    prior = passed_along(clip_video, "ts", 1)
    opening = lax.axis_index("ts") == 0
    prior = jnp.where(opening, jnp.zeros_like(prior), prior)
    volume = jnp.concatenate([prior, clip_video], axis=0)
    whole_spatial, whole_temporal = side_by_side(
        (input_spatial, input_temporal), ("dp", "ts"), 0, 1
    )
    features = jax.nn.gelu(conv_local(volume, conv_weight, frames_here), approximate=True).astype(
        jnp.bfloat16
    )
    frames, height, columns, channels = features.shape
    places = height * columns
    tokens = frames * places
    embedded = jnp.dot(
        features.reshape(tokens, channels), embed_weight, preferred_element_type=jnp.float32
    ).astype(jnp.bfloat16)
    normed_one, factor_one = rms_norm(embedded, gain_spatial)
    packed_one = jnp.dot(normed_one, whole_spatial, preferred_element_type=jnp.float32).astype(
        jnp.bfloat16
    )
    packed_one = packed_one.reshape(frames, places, -1)
    mixture_one, attend_one = frame_forward(packed_one)
    after_space = (
        embedded.astype(jnp.float32)
        + jnp.dot(
            mixture_one.reshape(tokens, -1), output_spatial, preferred_element_type=jnp.float32
        )
    ).astype(jnp.bfloat16)
    normed_two, factor_two = rms_norm(after_space, gain_temporal)
    packed_two = jnp.dot(normed_two, whole_temporal, preferred_element_type=jnp.float32).astype(
        jnp.bfloat16
    )
    packed_two = packed_two.reshape(frames, places, -1)
    cotangent_rows = cotangent.reshape(tokens, -1)
    grad_mix_two = jnp.dot(
        cotangent_rows, output_temporal.T, preferred_element_type=jnp.float32
    ).astype(jnp.bfloat16)
    grad_mix_two = grad_mix_two.reshape(frames, places, -1)
    patched = lax.all_to_all(packed_two, "ts", split_axis=1, concat_axis=0, tiled=True)
    mixture_patched, attend_two = clip_forward(patched)
    mixture_two = lax.all_to_all(mixture_patched, "ts", split_axis=0, concat_axis=1, tiled=True)
    grad_patched = lax.all_to_all(grad_mix_two, "ts", split_axis=1, concat_axis=0, tiled=True)
    grad_packed_patched = clip_backward(patched, attend_two, grad_patched)
    grad_packed_two = lax.all_to_all(
        grad_packed_patched, "ts", split_axis=0, concat_axis=1, tiled=True
    )
    after_time = (
        after_space.astype(jnp.float32)
        + jnp.dot(
            mixture_two.reshape(tokens, -1), output_temporal, preferred_element_type=jnp.float32
        )
    ).astype(jnp.bfloat16)
    grad_packed_two = grad_packed_two.reshape(tokens, -1)
    grad_normed_two = jnp.dot(grad_packed_two, whole_temporal.T, preferred_element_type=jnp.float32)
    grad_after = (
        cotangent_rows.astype(jnp.float32)
        + rms_norm_grad(after_space, gain_temporal, factor_two, grad_normed_two)
    ).astype(jnp.bfloat16)
    grad_mix_one = jnp.dot(grad_after, output_spatial.T, preferred_element_type=jnp.float32).astype(
        jnp.bfloat16
    )
    grad_packed_one = frame_backward(
        packed_one, attend_one, grad_mix_one.reshape(frames, places, -1)
    ).reshape(tokens, -1)
    part_spatial = lax.dot_general(
        normed_one, grad_packed_one, (((0,), (0,)), ((), ())), preferred_element_type=jnp.float32
    )
    group_spatial = lax.psum_scatter(
        part_spatial.astype(jnp.bfloat16), "dp", scatter_dimension=0, tiled=True
    )
    grad_spatial = sum_at_owner(group_spatial, "ts", 0)
    return (after_time.reshape(frames, height, columns, -1), grad_spatial)


def solution(mesh):
    placed = (
        P(("dp", "ts"), None, None, None),
        P(),
        P(),
        P(),
        P(),
        P(("dp", "ts"), None),
        P(("dp", "ts"), None),
        P(),
        P(),
        P(("dp", "ts"), None, None, None),
    )
    return jax.shard_map(
        shards,
        mesh=mesh,
        in_specs=placed,
        out_specs=(P(("dp", "ts"), None, None, None), P(("dp", "ts"), None)),
        check_vma=False,
    )
```

profile of v0, /device:TPU:1, one launch (start us, length us, event | category | flops | bytes accessed | tf_op | source)
XLA Modules:
  0.0 364.3 jit_solution(13691863951065526166)
XLA Ops:
  7.2 1.5 maximum_bitcast_fusion
  8.7 4.6 %collective-permute-start = (bf16[2,4,40,128]{3,2,1,0:T(8,128)(2,1)}, bf16[2,4,40,128]{3,2,1,0:T(8,128)(2,1)S(1)}, u32[]{:S(2)}, u32[]{:S(2)}) collective-permute-start(bf16[2,4,40,128]{3,2,1,0:T(8,128)(2,1)} %param.10), channel_id=1, source_target_pairs={{0,1},{1,2},{2,3},{3,4},{4,5},{5,6},{6,7},{7,8},{8,9},{9,10},{10,1... | collective-permute-start | bytes 245768 | tf_op jit(solution)/shard_map/ppermute | solution.py:14
  13.3 3.4 convolution_convert_fusion.2
  16.7 0.7 copy.45
  17.4 8.5 %all-to-all-start.2 = ((bf16[2,160,128]{2,0,1:T(2,128)(2,1)}), bf16[2,160,128]{2,0,1:T(2,128)(2,1)S(1)}, u32[]{:S(2)}, u32[]{:S(2)}) async-start(bf16[2,160,128]{2,0,1:T(2,128)(2,1)} %copy.45), calls=%async_computation.2 | async-start | bytes 163840 | tf_op jit(solution)/shard_map/all_to_all | solution.py:212
  30.5 4.2 %fusion.4 = (f32[320]{0:T(512)S(1)}, bf16[320,5120]{1,0:T(8,128)(2,1)}) fusion(bf16[128,5120]{1,0:T(8,128)(2,1)} %param.12, f32[320,128]{1,0:T(8,128)S(1)} %convolution_add_fusion.1, bf16[320,128]{1,0:T(8,128)(2,1)S(1)} %bitcast.244, bf16[3,3,3,128,128]{4,3,2,1,0:T(8,128)(2,1)S(1)} %copy-done.5), kind=kOutput, calls=%fused_computation.15 | convolution fusion | flops 436879040 | bytes 4867328 | tf_op jit(solution)/shard_map/dot_general | solution.py:184
  34.7 100.0 %all-gather.3.cloned.1.call-done = bf16[256,20,768]{2,1,0:T(8,128)(2,1)} async-done(((bf16[1,20,768]{2,1,0:T(8,128)(2,1)}), bf16[256,20,768]{2,1,0:T(8,128)(2,1)}) %all-gather.3.cloned.1.call-update) | async-done | bytes 7864336 | tf_op jit(solution)/shard_map/all_gather | solution.py:20
  134.7 12.5 %reshape.220 = bf16[5120,768]{1,0:T(8,128)(2,1)} reshape(bf16[256,20,768]{2,1,0:T(8,128)(2,1)} %all-gather.3.cloned.1.call-done) | data formatting | bytes 15728640
  147.2 5.0 %fusion.26 = bf16[320,384]{1,0:T(8,128)(2,1)S(1)} fusion(bf16[5120,768]{1,0:T(8,128)(2,1)} %reshape.220, bf16[320,5120]{1,0:T(8,128)(2,1)} %get-tuple-element.32, f32[5120]{0:T(1024)S(1)} %copy-done.8, f32[320]{0:T(512)S(1)} %add_rsqrt_fusion.1), kind=kOutput, calls=%fused_computation.35 | convolution fusion | flops 1264967680 | bytes 7476480 | tf_op jit(solution)/shard_map/dot_general | solution.py:188
  152.2 0.3 fusion.182
  152.5 0.5 convolution_convert_fusion.6
  153.0 3.3 fusion.7
  156.3 5.2 %fusion.29 = bf16[320,384]{1,0:T(8,128)(2,1)S(1)} fusion(bf16[5120,768]{1,0:T(8,128)(2,1)} %reshape.220, bf16[320,5120]{1,0:T(8,128)(2,1)S(1)} %get-tuple-element.36, f32[5120]{0:T(1024)S(1)} %copy-done.7, f32[320]{0:T(512)S(1)} %get-tuple-element.30), kind=kOutput, calls=%fused_computation.36 | convolution fusion | flops 1264967680 | bytes 7476480 | tf_op jit(solution)/shard_map/dot_general | solution.py:200
  161.5 0.9 copy.36
  162.4 7.1 %all-to-all-start = ((bf16[2,160,384]{2,0,1:T(2,128)(2,1)}), bf16[2,160,384]{2,0,1:T(2,128)(2,1)S(1)}, u32[]{:S(2)}, u32[]{:S(2)}) async-start(bf16[2,160,384]{2,0,1:T(2,128)(2,1)} %copy.36), calls=%async_computation | async-start | bytes 491520 | tf_op jit(solution)/shard_map/all_to_all | solution.py:209
  169.7 10.6 %all-to-all-done = bf16[2,160,384]{2,0,1:T(2,128)(2,1)S(1)} async-done(((bf16[2,160,384]{2,0,1:T(2,128)(2,1)}), bf16[2,160,384]{2,0,1:T(2,128)(2,1)S(1)}, u32[]{:S(2)}, u32[]{:S(2)}) %all-to-all-start) | async-done | bytes 245792 | tf_op jit(solution)/shard_map/all_to_all | solution.py:209
  180.8 0.8 fusion.187
  182.6 17.4 %all_to_all.65 = bf16[64,5,384]{2,1,0:T(8,128)(2,1)S(1)} all-to-all(bf16[64,5,384]{2,1,0:T(8,128)(2,1)S(1)} %copy.53), channel_id=1, replica_groups=mesh['dp'=8,'ts'=32] {'ts'}, dimensions={0} | all-to-all | bytes 491520 | tf_op jit(solution)/shard_map/all_to_all | solution.py:214
  200.2 5.3 %fusion.14 = (f32[320]{0:T(512)S(1)}, f32[320,5120]{1,0:T(8,128)S(1)}) fusion(bf16[320,5120]{1,0:T(8,128)(2,1)} %copy-done.1, f32[5120]{0:T(1024)S(1)} %copy-done.7, bf16[320,384]{1,0:T(8,128)(2,1)S(1)} %reshape.216, bf16[5120,768]{1,0:T(8,128)(2,1)} %reshape.220), kind=kOutput, calls=%fused_computation.25 | convolution fusion | flops 1264844544 | bytes 14030080 | tf_op jit(solution)/shard_map/dot_general | solution.py:224
  205.5 2.0 fusion.41
  207.5 0.4 convolution_convert_fusion.4
  208.4 0.3 fusion.39
  208.6 6.6 %convolution_convert_fusion = bf16[5120,384]{1,0:T(8,128)(2,1)} fusion(bf16[320,5120]{1,0:T(8,128)(2,1)} %get-tuple-element.32, f32[5120]{0:T(1024)S(1)} %copy-done.8, f32[320]{0:T(512)S(1)} %add_rsqrt_fusion.1, bf16[320,128]{1,0:T(8,128)(2,1)S(1)} %bitcast.251, bf16[320,128]{1,0:T(8,128)(2,1)S(1)} %bitcast.252, bf16[320,128]{1,0:T(8,128)(2,1)S(1)} %bitcast.241), kind=kOutput, calls=%fused_computation.11 | convolution fusion | flops 1267548160 | bytes 7476480 | tf_op jit(solution)/shard_map/dot_general | solution.py:235
  215.3 0.2 fusion.46
  215.5 0.7 copy.43
  216.2 3.9 %all-to-all-start.1 = ((bf16[64,5,128]{2,1,0:T(8,128)(2,1)}), bf16[64,5,128]{2,1,0:T(8,128)(2,1)S(1)}, u32[]{:S(2)}, u32[]{:S(2)}) async-start(bf16[64,5,128]{2,1,0:T(8,128)(2,1)} %copy.43), calls=%async_computation.1 | async-start | bytes 262144 | tf_op jit(solution)/shard_map/all_to_all | solution.py:211
  220.2 109.8 %reduce-scatter.2.cloned.1.call-done = bf16[640,384]{1,0:T(8,128)(2,1)} async-done(((bf16[5120,384]{1,0:T(8,128)(2,1)}), bf16[640,384]{1,0:T(8,128)(2,1)}) %reduce-scatter.2.cloned.1.call-update) | async-done | bytes 491536 | tf_op jit(solution)/shard_map/reduce_scatter | solution.py:238
  330.0 1.9 reshape.218
  331.9 7.1 %all-to-all-start.4 = ((bf16[32,20,384]{2,1,0:T(8,128)(2,1)}), bf16[32,20,384]{2,1,0:T(8,128)(2,1)S(1)}, u32[]{:S(2)}, u32[]{:S(2)}) async-start(bf16[32,20,384]{2,1,0:T(8,128)(2,1)} %reshape.218), calls=%async_computation.5 | async-start | bytes 1179648 | tf_op jit(solution)/shard_map/all_to_all | solution.py:32
  339.1 4.6 %fusion.3 = bf16[320,5120]{1,0:T(8,128)(2,1)} fusion(bf16[320,128]{1,0:T(8,128)(2,1)S(1)} %reshape.211, bf16[128,5120]{1,0:T(8,128)(2,1)S(1)} %copy-done.4, bf16[320,5120]{1,0:T(8,128)(2,1)} %copy-done.1), kind=kOutput, calls=%fused_computation.13 | convolution fusion | flops 424345600 | bytes 7946240 | tf_op jit(solution)/shard_map/dot_general | solution.py:219
  343.7 13.0 %all-to-all-done.4 = bf16[32,20,384]{2,1,0:T(8,128)(2,1)S(1)} async-done(((bf16[32,20,384]{2,1,0:T(8,128)(2,1)}), bf16[32,20,384]{2,1,0:T(8,128)(2,1)S(1)}, u32[]{:S(2)}, u32[]{:S(2)}) %all-to-all-start.4) | async-done | bytes 491552 | tf_op jit(solution)/shard_map/all_to_all | solution.py:32
  356.7 0.7 convert_reduce_fusion
  (83 shorter events, 6.9 us)
Async XLA Ops:
  7.2 145.8 %copy-start = (bf16[128,5120]{1,0:T(8,128)(2,1)S(1)}, bf16[128,5120]{1,0:T(8,128)(2,1)}, u32[]{:S(2)}) copy-start(bf16[128,5120]{1,0:T(8,128)(2,1)} %param.17) | copy-start | bytes 3932164
  7.2 18.8 %copy-start.6 = (bf16[2,4,40,128]{3,2,1,0:T(8,128)(2,1)S(1)}, bf16[2,4,40,128]{3,2,1,0:T(8,128)(2,1)}, u32[]{:S(2)}) copy-start(bf16[2,4,40,128]{3,2,1,0:T(8,128)(2,1)} %param.10) | copy-start | bytes 245764
  7.2 127.5 %all-gather.3.cloned.1.call-start = ((), (), s32[]{:S(2)}) async-start(), calls=%async_computation.7 | async-start | bytes 9474048 | tf_op jit(solution)/shard_map/all_gather | solution.py:20
  8.7 17.2 %collective-permute-start = (bf16[2,4,40,128]{3,2,1,0:T(8,128)(2,1)}, bf16[2,4,40,128]{3,2,1,0:T(8,128)(2,1)S(1)}, u32[]{:S(2)}, u32[]{:S(2)}) collective-permute-start(bf16[2,4,40,128]{3,2,1,0:T(8,128)(2,1)} %param.10), channel_id=1, source_target_pairs={{0,1},{1,2},{2,3},{3,4},{4,5},{5,6},{6,7},{7,8},{8,9},{9,10},{10,1... | collective-permute-start | bytes 245768 | tf_op jit(solution)/shard_map/ppermute | solution.py:14
  13.3 13.0 %copy-start.5 = (bf16[3,3,3,128,128]{4,3,2,1,0:T(8,128)(2,1)S(1)}, bf16[3,3,3,128,128]{4,3,2,1,0:T(8,128)(2,1)}, u32[]{:S(2)}) copy-start(bf16[3,3,3,128,128]{4,3,2,1,0:T(8,128)(2,1)} %param.11) | copy-start | bytes 2654212
  17.4 145.0 %all-to-all-start.2 = ((bf16[2,160,128]{2,0,1:T(2,128)(2,1)}), bf16[2,160,128]{2,0,1:T(2,128)(2,1)S(1)}, u32[]{:S(2)}, u32[]{:S(2)}) async-start(bf16[2,160,128]{2,0,1:T(2,128)(2,1)} %copy.45), calls=%async_computation.2 | async-start | bytes 163840 | tf_op jit(solution)/shard_map/all_to_all | solution.py:212
  34.7 112.5 %copy-start.8 = (f32[5120]{0:T(1024)S(1)}, f32[5120]{0:T(1024)}, u32[]{:S(2)}) copy-start(f32[5120]{0:T(1024)} %param.13) | copy-start | bytes 61444
  153.0 3.3 copy-start.7
  156.2 5.3 %copy-start.1 = (bf16[320,5120]{1,0:T(8,128)(2,1)}, bf16[320,5120]{1,0:T(8,128)(2,1)S(1)}, u32[]{:S(2)}) copy-start(bf16[320,5120]{1,0:T(8,128)(2,1)S(1)} %get-tuple-element.36) | copy-start | bytes 9830404
  162.4 17.8 %all-to-all-start = ((bf16[2,160,384]{2,0,1:T(2,128)(2,1)}), bf16[2,160,384]{2,0,1:T(2,128)(2,1)S(1)}, u32[]{:S(2)}, u32[]{:S(2)}) async-start(bf16[2,160,384]{2,0,1:T(2,128)(2,1)} %copy.36), calls=%async_computation | async-start | bytes 491520 | tf_op jit(solution)/shard_map/all_to_all | solution.py:209
  169.5 160.4 %reduce-scatter.2.cloned.1.call-start = ((), (), s32[]{:S(2)}) async-start(), calls=%async_computation.6 | async-start | bytes 4423680 | tf_op jit(solution)/shard_map/reduce_scatter | solution.py:238
  200.2 5.3 %copy-start.2 = (bf16[320,5120]{1,0:T(8,128)(2,1)S(1)}, bf16[320,5120]{1,0:T(8,128)(2,1)}, u32[]{:S(2)}) copy-start(bf16[320,5120]{1,0:T(8,128)(2,1)} %copy-done.1) | copy-start | bytes 9830404
  200.2 5.3 %copy-start.3 = (bf16[2,4,40,5120]{3,2,1,0:T(8,128)(2,1)S(1)}, bf16[2,4,40,5120]{3,2,1,0:T(8,128)(2,1)}, u32[]{:S(2)}) copy-start(bf16[2,4,40,5120]{3,2,1,0:T(8,128)(2,1)} %param.19) | copy-start | bytes 9830404
  215.2 123.9 %copy-start.4 = (bf16[128,5120]{1,0:T(8,128)(2,1)S(1)}, bf16[128,5120]{1,0:T(8,128)(2,1)}, u32[]{:S(2)}) copy-start(bf16[128,5120]{1,0:T(8,128)(2,1)} %param.18) | copy-start | bytes 3932164
  216.2 115.7 %all-to-all-start.1 = ((bf16[64,5,128]{2,1,0:T(8,128)(2,1)}), bf16[64,5,128]{2,1,0:T(8,128)(2,1)S(1)}, u32[]{:S(2)}, u32[]{:S(2)}) async-start(bf16[64,5,128]{2,1,0:T(8,128)(2,1)} %copy.43), calls=%async_computation.1 | async-start | bytes 262144 | tf_op jit(solution)/shard_map/all_to_all | solution.py:211
  331.9 24.8 %all-to-all-start.4 = ((bf16[32,20,384]{2,1,0:T(8,128)(2,1)}), bf16[32,20,384]{2,1,0:T(8,128)(2,1)S(1)}, u32[]{:S(2)}, u32[]{:S(2)}) async-start(bf16[32,20,384]{2,1,0:T(8,128)(2,1)} %reshape.218), calls=%async_computation.5 | async-start | bytes 1179648 | tf_op jit(solution)/shard_map/all_to_all | solution.py:32
Sparse Core Ops, SparseCore 0:
  12.3 122.3 all-gather.2
  215.4 114.5 reduce-scatter.1
where the time goes:
time: 365 us; the launch traced here: 364 us
  waiting for transfers between devices  233 us (64%)
  matrix products  46.7 us (13%)
  starting transfers between devices  31.3 us (9%)
  local copies, waits for them, and re-layouts  17.8 us (5%)
  blocking collectives  17.4 us (5%)
  between operations  14.5 us (4%)
    reduce_scatter x1, waiting for transfers between devices, shards(): lax.psum_scatter(part_spatial.astype(jnp.bfloat16), 'dp', scatter_dimensi...  110 us
    all_gather x1, waiting for transfers between devices, side_by_side(): whole = lax.all_gather(both, axis, axis=dim, tiled=True)  100 us
    all_to_all x1, blocking collectives, shards(): lax.all_to_all(grad_packed_patched, 'ts', split_axis=0, concat_axis=1, ti...  17.4 us
    all_to_all x1, waiting for transfers between devices, sum_at_owner(): lax.all_to_all(parts, axis, split_axis=0, concat_axis=0, tiled=True)  13 us
    unnamed x19, local copies, waits for them, and re-layouts  12.5 us
    all_to_all x1, waiting for transfers between devices, shards(): lax.all_to_all(packed_two, 'ts', split_axis=1, concat_axis=0, tiled=True)  10.6 us
    all_to_all x1, starting transfers between devices, shards(): lax.all_to_all(grad_mix_two, 'ts', split_axis=1, concat_axis=0, tiled=True)  8.51 us
  transfers between devices with their start and end apart: 7, of which 4 were waited for; matrix products, arithmetic and copies ran while one was open for 13% of the time, Pallas kernels for 0%

commit v1 on v0

--- a/solution.py
+++ b/solution.py
@@ -209,7 +209,15 @@
     patched = lax.all_to_all(packed_two, "ts", split_axis=1, concat_axis=0, tiled=True)
     mixture_patched, attend_two = clip_forward(patched)
     mixture_two = lax.all_to_all(mixture_patched, "ts", split_axis=0, concat_axis=1, tiled=True)
-    grad_patched = lax.all_to_all(grad_mix_two, "ts", split_axis=1, concat_axis=0, tiled=True)
+    grad_patched = jnp.concatenate(
+        lax.all_to_all(
+            jnp.stack(jnp.split(grad_mix_two, lax.axis_size("ts"), axis=1), axis=0),
+            axis_name="ts",
+            split_axis=0,
+            concat_axis=0,
+        ),
+        axis=0,
+    )
     grad_packed_patched = clip_backward(patched, attend_two, grad_patched)
     grad_packed_two = lax.all_to_all(
         grad_packed_patched, "ts", split_axis=0, concat_axis=1, tiled=True

time: 365 us -> 365 us (level)
  local copies, waits for them, and re-layouts: 17.8 us -> 36 us
  waiting for transfers between devices: 233 us -> 215 us
    unnamed x19 -> x50, local copies, waits for them, and re-layouts: 12.5 us -> 30.7 us
    all_gather x1, waiting for transfers between devices: 100 us -> 81.9 us  [side_by_side(): whole = lax.all_gather(both, axis, axis=dim, tiled=True)]
  transfers between devices with their start and end apart: 7 -> 7, of which waited for: 4 -> 4; matrix products, arithmetic and copies ran while one was open for 13% -> 18% of each run, Pallas kernels for 0% -> 0%
where the time goes in v1:
time: 365 us; the launch traced here: 364 us
  waiting for transfers between devices  215 us (59%)
  matrix products  46.7 us (13%)
  local copies, waits for them, and re-layouts  36 us (10%)
  starting transfers between devices  31.3 us (9%)
  blocking collectives  17.4 us (5%)
  between operations  14.5 us (4%)
    reduce_scatter x1, waiting for transfers between devices, shards(): lax.psum_scatter(part_spatial.astype(jnp.bfloat16), 'dp', scatter_dimensi...  110 us
    all_gather x1, waiting for transfers between devices, side_by_side(): whole = lax.all_gather(both, axis, axis=dim, tiled=True)  81.9 us
    unnamed x50, local copies, waits for them, and re-layouts  30.7 us
    all_to_all x1, blocking collectives, shards(): lax.all_to_all(grad_packed_patched, 'ts', split_axis=0, concat_axis=1, ti...  17.4 us
    all_to_all x1, waiting for transfers between devices, sum_at_owner(): lax.all_to_all(parts, axis, split_axis=0, concat_axis=0, tiled=True)  13 us
    all_to_all x1, waiting for transfers between devices, shards(): lax.all_to_all(packed_two, 'ts', split_axis=1, concat_axis=0, tiled=True)  10.6 us
    all_to_all x1, starting transfers between devices, shards(): lax.all_to_all(jnp.stack(jnp.split(grad_mix_two, lax.axis_size('ts'), axi...  8.51 us
  transfers between devices with their start and end apart: 7, of which 4 were waited for; matrix products, arithmetic and copies ran while one was open for 18% of the time, Pallas kernels for 0%

profile of v1, /device:TPU:1, one launch (start us, length us, event | category | flops | bytes accessed | tf_op | source)
XLA Modules:
  0.0 364.4 jit_solution(16975596645708631721)
XLA Ops:
  7.2 1.5 maximum_bitcast_fusion
  8.7 4.6 %collective-permute-start = (bf16[2,4,40,128]{3,2,1,0:T(8,128)(2,1)}, bf16[2,4,40,128]{3,2,1,0:T(8,128)(2,1)S(1)}, u32[]{:S(2)}, u32[]{:S(2)}) collective-permute-start(bf16[2,4,40,128]{3,2,1,0:T(8,128)(2,1)} %param.10), channel_id=1, source_target_pairs={{0,1},{1,2},{2,3},{3,4},{4,5},{5,6},{6,7},{7,8},{8,9},{9,10},{10,1... | collective-permute-start | bytes 245768 | tf_op jit(solution)/shard_map/ppermute | solution.py:14
  13.3 3.4 convolution_convert_fusion.2
  20.3 0.6 constant_dynamic-update-slice_fusion.25
  23.8 0.6 constant_dynamic-update-slice_fusion.19
  24.4 0.6 constant_dynamic-update-slice_fusion.18
  27.4 0.6 constant_dynamic-update-slice_fusion.13
  28.5 0.6 constant_dynamic-update-slice_fusion.11
  35.0 0.6 constant_dynamic-update-slice_fusion
  35.6 8.5 %all-to-all-start.2 = ((bf16[32,2,5,128]{3,1,2,0:T(2,128)(2,1)}), bf16[32,2,5,128]{3,1,2,0:T(2,128)(2,1)S(1)}, u32[]{:S(2)}, u32[]{:S(2)}) async-start(bf16[32,2,5,128]{3,1,2,0:T(2,128)(2,1)} %constant_dynamic-update-slice_fusion), calls=%async_computation.2 | async-start | bytes 163840 | tf_op jit(solution)/shard_map/all_to_all | solution.py:213
  48.7 4.2 %fusion.4 = (f32[320]{0:T(512)S(1)}, bf16[320,5120]{1,0:T(8,128)(2,1)}) fusion(bf16[128,5120]{1,0:T(8,128)(2,1)} %param.12, f32[320,128]{1,0:T(8,128)S(1)} %convolution_add_fusion.1, bf16[320,128]{1,0:T(8,128)(2,1)S(1)} %bitcast.369, bf16[3,3,3,128,128]{4,3,2,1,0:T(8,128)(2,1)S(1)} %copy-done.5), kind=kOutput, calls=%fused_computation.15 | convolution fusion | flops 436879040 | bytes 4867328 | tf_op jit(solution)/shard_map/dot_general | solution.py:184
  52.9 81.9 %all-gather.3.cloned.1.call-done = bf16[256,20,768]{2,1,0:T(8,128)(2,1)} async-done(((bf16[1,20,768]{2,1,0:T(8,128)(2,1)}), bf16[256,20,768]{2,1,0:T(8,128)(2,1)}) %all-gather.3.cloned.1.call-update) | async-done | bytes 7864336 | tf_op jit(solution)/shard_map/all_gather | solution.py:20
  134.8 12.5 %reshape.215 = bf16[5120,768]{1,0:T(8,128)(2,1)} reshape(bf16[256,20,768]{2,1,0:T(8,128)(2,1)} %all-gather.3.cloned.1.call-done) | data formatting | bytes 15728640
  147.3 5.0 %fusion.26 = bf16[320,384]{1,0:T(8,128)(2,1)S(1)} fusion(bf16[5120,768]{1,0:T(8,128)(2,1)} %reshape.215, bf16[320,5120]{1,0:T(8,128)(2,1)} %get-tuple-element.64, f32[5120]{0:T(1024)S(1)} %copy-done.8, f32[320]{0:T(512)S(1)} %add_rsqrt_fusion.1), kind=kOutput, calls=%fused_computation.35 | convolution fusion | flops 1264967680 | bytes 7476480 | tf_op jit(solution)/shard_map/dot_general | solution.py:188
  153.1 3.3 fusion.7
  156.4 5.2 %fusion.29 = bf16[320,384]{1,0:T(8,128)(2,1)S(1)} fusion(bf16[5120,768]{1,0:T(8,128)(2,1)} %reshape.215, bf16[320,5120]{1,0:T(8,128)(2,1)S(1)} %get-tuple-element.68, f32[5120]{0:T(1024)S(1)} %copy-done.7, f32[320]{0:T(512)S(1)} %get-tuple-element.62), kind=kOutput, calls=%fused_computation.36 | convolution fusion | flops 1264967680 | bytes 7476480 | tf_op jit(solution)/shard_map/dot_general | solution.py:200
  161.6 0.9 copy.66
  162.5 7.1 %all-to-all-start = ((bf16[2,160,384]{2,0,1:T(2,128)(2,1)}), bf16[2,160,384]{2,0,1:T(2,128)(2,1)S(1)}, u32[]{:S(2)}, u32[]{:S(2)}) async-start(bf16[2,160,384]{2,0,1:T(2,128)(2,1)} %copy.66), calls=%async_computation | async-start | bytes 491520 | tf_op jit(solution)/shard_map/all_to_all | solution.py:209
  169.8 10.6 %all-to-all-done = bf16[2,160,384]{2,0,1:T(2,128)(2,1)S(1)} async-done(((bf16[2,160,384]{2,0,1:T(2,128)(2,1)}), bf16[2,160,384]{2,0,1:T(2,128)(2,1)S(1)}, u32[]{:S(2)}, u32[]{:S(2)}) %all-to-all-start) | async-done | bytes 245792 | tf_op jit(solution)/shard_map/all_to_all | solution.py:209
  180.9 0.8 fusion.189
  182.7 17.4 %all_to_all.55 = bf16[64,5,384]{2,1,0:T(8,128)(2,1)S(1)} all-to-all(bf16[64,5,384]{2,1,0:T(8,128)(2,1)S(1)} %copy.114), channel_id=1, replica_groups=mesh['dp'=8,'ts'=32] {'ts'}, dimensions={0} | all-to-all | bytes 491520 | tf_op jit(solution)/shard_map/all_to_all | solution.py:222
  200.3 5.3 %fusion.14 = (f32[320]{0:T(512)S(1)}, f32[320,5120]{1,0:T(8,128)S(1)}) fusion(bf16[320,5120]{1,0:T(8,128)(2,1)} %copy-done.1, f32[5120]{0:T(1024)S(1)} %copy-done.7, bf16[320,384]{1,0:T(8,128)(2,1)S(1)} %reshape.211, bf16[5120,768]{1,0:T(8,128)(2,1)} %reshape.215), kind=kOutput, calls=%fused_computation.25 | convolution fusion | flops 1264844544 | bytes 14030080 | tf_op jit(solution)/shard_map/dot_general | solution.py:232
  205.6 2.0 fusion.41
  208.7 6.6 %convolution_convert_fusion = bf16[5120,384]{1,0:T(8,128)(2,1)} fusion(bf16[320,5120]{1,0:T(8,128)(2,1)} %get-tuple-element.64, f32[5120]{0:T(1024)S(1)} %copy-done.8, f32[320]{0:T(512)S(1)} %add_rsqrt_fusion.1, bf16[320,128]{1,0:T(8,128)(2,1)S(1)} %bitcast.376, bf16[320,128]{1,0:T(8,128)(2,1)S(1)} %bitcast.377, bf16[320,128]{1,0:T(8,128)(2,1)S(1)} %bitcast.366), kind=kOutput, calls=%fused_computation.11 | convolution fusion | flops 1267548160 | bytes 7476480 | tf_op jit(solution)/shard_map/dot_general | solution.py:243
  215.6 0.7 copy.73
  216.3 4.0 %all-to-all-start.1 = ((bf16[64,5,128]{2,1,0:T(8,128)(2,1)}), bf16[64,5,128]{2,1,0:T(8,128)(2,1)S(1)}, u32[]{:S(2)}, u32[]{:S(2)}) async-start(bf16[64,5,128]{2,1,0:T(8,128)(2,1)} %copy.73), calls=%async_computation.1 | async-start | bytes 262144 | tf_op jit(solution)/shard_map/all_to_all | solution.py:211
  220.3 109.8 %reduce-scatter.2.cloned.1.call-done = bf16[640,384]{1,0:T(8,128)(2,1)} async-done(((bf16[5120,384]{1,0:T(8,128)(2,1)}), bf16[640,384]{1,0:T(8,128)(2,1)}) %reduce-scatter.2.cloned.1.call-update) | async-done | bytes 491536 | tf_op jit(solution)/shard_map/reduce_scatter | solution.py:246
  330.1 1.9 reshape.213
  332.0 7.0 %all-to-all-start.4 = ((bf16[32,20,384]{2,1,0:T(8,128)(2,1)}), bf16[32,20,384]{2,1,0:T(8,128)(2,1)S(1)}, u32[]{:S(2)}, u32[]{:S(2)}) async-start(bf16[32,20,384]{2,1,0:T(8,128)(2,1)} %reshape.213), calls=%async_computation.5 | async-start | bytes 1179648 | tf_op jit(solution)/shard_map/all_to_all | solution.py:32
  339.2 4.6 %fusion.3 = bf16[320,5120]{1,0:T(8,128)(2,1)} fusion(bf16[320,128]{1,0:T(8,128)(2,1)S(1)} %reshape.207, bf16[128,5120]{1,0:T(8,128)(2,1)S(1)} %copy-done.4, bf16[320,5120]{1,0:T(8,128)(2,1)} %copy-done.1), kind=kOutput, calls=%fused_computation.13 | convolution fusion | flops 424345600 | bytes 7946240 | tf_op jit(solution)/shard_map/dot_general | solution.py:227
  343.8 13.0 %all-to-all-done.4 = bf16[32,20,384]{2,1,0:T(8,128)(2,1)S(1)} async-done(((bf16[32,20,384]{2,1,0:T(8,128)(2,1)}), bf16[32,20,384]{2,1,0:T(8,128)(2,1)S(1)}, u32[]{:S(2)}, u32[]{:S(2)}) %all-to-all-start.4) | async-done | bytes 491552 | tf_op jit(solution)/shard_map/all_to_all | solution.py:32
  356.8 0.7 convert_reduce_fusion
  (116 shorter events, 23.9 us)
Async XLA Ops:
  7.2 145.9 %copy-start = (bf16[128,5120]{1,0:T(8,128)(2,1)S(1)}, bf16[128,5120]{1,0:T(8,128)(2,1)}, u32[]{:S(2)}) copy-start(bf16[128,5120]{1,0:T(8,128)(2,1)} %param.17) | copy-start | bytes 3932164
  7.2 37.0 %copy-start.6 = (bf16[2,4,40,128]{3,2,1,0:T(8,128)(2,1)S(1)}, bf16[2,4,40,128]{3,2,1,0:T(8,128)(2,1)}, u32[]{:S(2)}) copy-start(bf16[2,4,40,128]{3,2,1,0:T(8,128)(2,1)} %param.10) | copy-start | bytes 245764
  7.2 127.6 %all-gather.3.cloned.1.call-start = ((), (), s32[]{:S(2)}) async-start(), calls=%async_computation.7 | async-start | bytes 9474048 | tf_op jit(solution)/shard_map/all_gather | solution.py:20
  8.7 35.4 %collective-permute-start = (bf16[2,4,40,128]{3,2,1,0:T(8,128)(2,1)}, bf16[2,4,40,128]{3,2,1,0:T(8,128)(2,1)S(1)}, u32[]{:S(2)}, u32[]{:S(2)}) collective-permute-start(bf16[2,4,40,128]{3,2,1,0:T(8,128)(2,1)} %param.10), channel_id=1, source_target_pairs={{0,1},{1,2},{2,3},{3,4},{4,5},{5,6},{6,7},{7,8},{8,9},{9,10},{10,1... | collective-permute-start | bytes 245768 | tf_op jit(solution)/shard_map/ppermute | solution.py:14
  13.3 31.2 %copy-start.5 = (bf16[3,3,3,128,128]{4,3,2,1,0:T(8,128)(2,1)S(1)}, bf16[3,3,3,128,128]{4,3,2,1,0:T(8,128)(2,1)}, u32[]{:S(2)}) copy-start(bf16[3,3,3,128,128]{4,3,2,1,0:T(8,128)(2,1)} %param.11) | copy-start | bytes 2654212
  35.6 126.9 %all-to-all-start.2 = ((bf16[32,2,5,128]{3,1,2,0:T(2,128)(2,1)}), bf16[32,2,5,128]{3,1,2,0:T(2,128)(2,1)S(1)}, u32[]{:S(2)}, u32[]{:S(2)}) async-start(bf16[32,2,5,128]{3,1,2,0:T(2,128)(2,1)} %constant_dynamic-update-slice_fusion), calls=%async_computation.2 | async-start | bytes 163840 | tf_op jit(solution)/shard_map/all_to_all | solution.py:213
  52.9 94.4 %copy-start.8 = (f32[5120]{0:T(1024)S(1)}, f32[5120]{0:T(1024)}, u32[]{:S(2)}) copy-start(f32[5120]{0:T(1024)} %param.13) | copy-start | bytes 61444
  153.1 3.3 copy-start.7
  156.3 5.2 %copy-start.1 = (bf16[320,5120]{1,0:T(8,128)(2,1)}, bf16[320,5120]{1,0:T(8,128)(2,1)S(1)}, u32[]{:S(2)}) copy-start(bf16[320,5120]{1,0:T(8,128)(2,1)S(1)} %get-tuple-element.68) | copy-start | bytes 9830404
  162.5 17.9 %all-to-all-start = ((bf16[2,160,384]{2,0,1:T(2,128)(2,1)}), bf16[2,160,384]{2,0,1:T(2,128)(2,1)S(1)}, u32[]{:S(2)}, u32[]{:S(2)}) async-start(bf16[2,160,384]{2,0,1:T(2,128)(2,1)} %copy.66), calls=%async_computation | async-start | bytes 491520 | tf_op jit(solution)/shard_map/all_to_all | solution.py:209
  169.6 160.5 %reduce-scatter.2.cloned.1.call-start = ((), (), s32[]{:S(2)}) async-start(), calls=%async_computation.6 | async-start | bytes 4423680 | tf_op jit(solution)/shard_map/reduce_scatter | solution.py:246
  200.3 5.3 %copy-start.2 = (bf16[320,5120]{1,0:T(8,128)(2,1)S(1)}, bf16[320,5120]{1,0:T(8,128)(2,1)}, u32[]{:S(2)}) copy-start(bf16[320,5120]{1,0:T(8,128)(2,1)} %copy-done.1) | copy-start | bytes 9830404
  200.3 5.3 %copy-start.3 = (bf16[2,4,40,5120]{3,2,1,0:T(8,128)(2,1)S(1)}, bf16[2,4,40,5120]{3,2,1,0:T(8,128)(2,1)}, u32[]{:S(2)}) copy-start(bf16[2,4,40,5120]{3,2,1,0:T(8,128)(2,1)} %param.19) | copy-start | bytes 9830404
  215.3 123.9 %copy-start.4 = (bf16[128,5120]{1,0:T(8,128)(2,1)S(1)}, bf16[128,5120]{1,0:T(8,128)(2,1)}, u32[]{:S(2)}) copy-start(bf16[128,5120]{1,0:T(8,128)(2,1)} %param.18) | copy-start | bytes 3932164
  216.3 115.7 %all-to-all-start.1 = ((bf16[64,5,128]{2,1,0:T(8,128)(2,1)}), bf16[64,5,128]{2,1,0:T(8,128)(2,1)S(1)}, u32[]{:S(2)}, u32[]{:S(2)}) async-start(bf16[64,5,128]{2,1,0:T(8,128)(2,1)} %copy.73), calls=%async_computation.1 | async-start | bytes 262144 | tf_op jit(solution)/shard_map/all_to_all | solution.py:211
  332.0 24.8 %all-to-all-start.4 = ((bf16[32,20,384]{2,1,0:T(8,128)(2,1)}), bf16[32,20,384]{2,1,0:T(8,128)(2,1)S(1)}, u32[]{:S(2)}, u32[]{:S(2)}) async-start(bf16[32,20,384]{2,1,0:T(8,128)(2,1)} %reshape.213), calls=%async_computation.5 | async-start | bytes 1179648 | tf_op jit(solution)/shard_map/all_to_all | solution.py:32
Sparse Core Ops, SparseCore 0:
  12.3 122.4 all-gather.2
  215.4 114.6 reduce-scatter.1
